TPU v7x, 32 devices: a whole 2x2x4 slice. The times are simulated.
32 devices in a mesh: dom: 8 (over y, x, core), tp: 4 (over z).
Axes of the slice: x: 2, y: 2, z: 4, core: 2. Of those that a mesh axis runs over, the one named last changes fastest.
Arguments:
- activations: bfloat16 [4, 128, 4096], P(None, 'dom', 'tp'), may hold values from -6 to 6
- norm_gain: float32 [4096], replicated, may hold values from 0.5 to 1.5
- w_query: bfloat16 [4096, 4096], P(None, 'tp'), may hold values from -0.09375 to 0.09375
- w_key: bfloat16 [4096, 1024], P(None, 'tp'), may hold values from -0.09375 to 0.09375
- value_weight: bfloat16 [4096, 1024], P(None, 'tp'), may hold values from -0.5 to 0.5
- w_output: bfloat16 [4096, 4096], P('tp'), may hold values from -0.09375 to 0.09375
- cache_keys: bfloat16 [128, 128, 1024], P('dom', None, 'tp'), may hold values from -740 to 740
- cache_values: bfloat16 [128, 128, 1024], P('dom', None, 'tp'), may hold values from -48 to 48
- tokens: int32 [4, 128], P(None, 'dom'), may hold values from 0 to 128255
- twisting_table: bfloat16 [128256], replicated, may hold values from -6 to 6
- twist_vec: float32 [4096], P('tp'), may hold values from -0.09375 to 0.09375
- previous_log_weights: float32 [128], P('dom'), may hold values from -300 to 0
- copy_counts: int32 [128], P('dom'), may hold values from 0 to 4, as said below
Outputs:
- attn_out: bfloat16 [4, 128, 4096], P(None, 'dom', 'tp')
- new_keys: bfloat16 [128, 132, 1024], P('dom', None, 'tp')
- new_values: bfloat16 [128, 132, 1024], P('dom', None, 'tp')
- out_logw: float32 [128], P('dom')
Inputs may be any that keep to these rules, and one draw needn't show every extreme that they name: copy_counts sum to 128; the particles of one index of dom have together at most 64 copies, and one index has exactly that many.
All inputs are finite; a program needn't handle non-finite values.
Results may differ from a plain program's by a relative error of at most 0.012.
The roundings to bfloat16 on the way count: a program that leaves them out, or rounds other values in their place, can miss the bound.
Values may be sent and summed in bfloat16 or wider, within the bound.
A program may use at most 128 MiB of HBM per device.

v0:
```python
import jax
import jax.numpy as jnp
from jax import lax
from jax.sharding import PartitionSpec as P

D = 4096
HD = 128


def entering(part, axis, combine, identity):
    place = lax.axis_index(axis)
    gathered = lax.all_gather(part, axis)
    state = jnp.zeros_like(part) + jnp.asarray(identity, part.dtype)

    def one(lap, state):
        return combine(state, lax.dynamic_index_in_dim(gathered, lap, 0, False))

    return lax.fori_loop(0, place, one, state)


def rotate(tensor, positions):
    middle = tensor.shape[-1] // 2
    frequency = 500000.0 ** (-2.0 * jnp.arange(middle, dtype=jnp.float32) / tensor.shape[-1])
    angles = positions[:, None] * frequency[None, :]
    cosine = jnp.cos(angles)[:, None, None, :]
    sine_part = jnp.sin(angles)[:, None, None, :]
    lower_half = tensor[..., :middle]
    upper_half = tensor[..., middle:]
    return jnp.concatenate(
        [
            lower_half * cosine - upper_half * sine_part,
            upper_half * cosine + lower_half * sine_part,
        ],
        -1,
    )


def add_counts(former, latter):
    return former + latter


def local(
    activations,
    norm_gain,
    w_query,
    w_key,
    value_weight,
    w_output,
    cache_keys,
    cache_values,
    tokens,
    twisting_table,
    twist_vec,
    previous_log_weights,
    copy_counts,
):
    step_count = activations.shape[0]
    particle_count = activations.shape[1]
    span_old = cache_keys.shape[1]
    dom_size = lax.axis_size("dom")
    kv_local = w_key.shape[1] // HD
    q_local = w_query.shape[1] // HD
    group_size = q_local // kv_local
    capacity = 4 * particle_count // dom_size
    total_copies = jnp.sum(copy_counts)
    offset = entering(total_copies, "dom", add_counts, jnp.int32(0))
    starts = jnp.cumsum(copy_counts) - copy_counts
    position = jnp.arange(dom_size * capacity, dtype=jnp.int32)
    target = position // capacity
    copy_rank = position % capacity * dom_size + (target - offset) % dom_size
    is_live = copy_rank < total_copies
    source = jnp.sum((starts[None, :] <= copy_rank[:, None]).astype(jnp.int32), 1) - 1
    arrival = jnp.where(is_live, (offset + copy_rank) // dom_size, particle_count).astype(
        jnp.bfloat16
    )

    def pack_rows(tensor):
        return jnp.where(is_live[:, None, None], tensor[source], jnp.zeros((), tensor.dtype))

    def place_rows(tensor, slot_index):
        blank = jnp.zeros((particle_count,) + tensor.shape[1:], tensor.dtype)
        return blank.at[slot_index].set(tensor, mode="drop")

    gathered = lax.all_gather(activations, "tp", axis=2, tiled=True)
    inputs = gathered.astype(jnp.float32)
    normed = (
        inputs * lax.rsqrt(jnp.mean(inputs * inputs, -1, keepdims=True) + 1e-05) * norm_gain
    ).astype(jnp.bfloat16)
    flat_rows = normed.reshape(step_count * particle_count, D)
    positions = (span_old + jnp.arange(step_count, dtype=jnp.int32)).astype(jnp.float32)
    queries = jnp.dot(flat_rows, w_query, preferred_element_type=jnp.float32).reshape(
        step_count, particle_count, q_local, HD
    )
    queries = rotate(queries, positions).astype(jnp.bfloat16)
    fresh_keys = jnp.dot(flat_rows, w_key, preferred_element_type=jnp.float32).reshape(
        step_count, particle_count, kv_local, HD
    )
    fresh_keys = (
        rotate(fresh_keys, positions)
        .astype(jnp.bfloat16)
        .reshape(step_count, particle_count, kv_local * HD)
    )
    fresh_values = jnp.dot(flat_rows, value_weight, preferred_element_type=jnp.float32).astype(
        jnp.bfloat16
    )
    fresh_values = fresh_values.reshape(step_count, particle_count, kv_local * HD)
    fresh_keys = jnp.transpose(fresh_keys, (1, 0, 2))
    fresh_values = jnp.transpose(fresh_values, (1, 0, 2))
    key_rows = jnp.concatenate([cache_keys, fresh_keys], 1)
    value_rows = jnp.concatenate([cache_values, fresh_values], 1)
    key_span = span_old + step_count
    query_heads = queries.reshape(step_count, particle_count, kv_local, group_size, HD)
    key_heads = key_rows.reshape(particle_count, key_span, kv_local, HD)
    value_heads = value_rows.reshape(particle_count, key_span, kv_local, HD)
    scores = (
        jnp.einsum("snkgd,nlkd->snkgl", query_heads, key_heads, preferred_element_type=jnp.float32)
        / HD**0.5
    )
    allowed = (
        jnp.arange(key_span, dtype=jnp.int32)[None, :]
        <= (span_old + jnp.arange(step_count, dtype=jnp.int32))[:, None]
    )
    allowed = allowed[:, None, None, None, :]
    masked = jnp.where(allowed, scores, -jnp.inf)
    highest = jnp.max(masked, -1, keepdims=True)
    exponent = jnp.exp(masked - highest)
    weights = (exponent / jnp.sum(exponent, -1, keepdims=True)).astype(jnp.bfloat16)
    context = jnp.einsum(
        "snkgl,nlkd->snkgd", weights, value_heads, preferred_element_type=jnp.float32
    ).astype(jnp.bfloat16)
    context = context.reshape(step_count * particle_count, q_local * HD)
    partial_value = jnp.dot(context, w_output, preferred_element_type=jnp.float32).reshape(
        step_count, particle_count, D
    )
    head_mix = lax.psum_scatter(partial_value, "tp", scatter_dimension=2, tiled=True)
    attn_out = head_mix.astype(jnp.bfloat16)
    summed = activations.astype(jnp.float32) + head_mix
    aligned, energy = lax.psum(
        (jnp.sum(summed * twist_vec, -1), jnp.sum(summed * summed, -1)), "tp"
    )
    twisting_score = aligned / jnp.sqrt(energy / D + 1e-06)
    token_reward = twisting_table[tokens].astype(jnp.float32)
    particle_log_weight = previous_log_weights + jnp.sum(token_reward + twisting_score, 0)
    largest = lax.pmax(jnp.max(particle_log_weight), "dom")
    mass_total = lax.psum(jnp.sum(jnp.exp(particle_log_weight - largest)), "dom")
    out_logw = particle_log_weight - (largest + jnp.log(mass_total))
    moved_keys, moved_values, arrived = (
        lax.all_to_all(pack_rows(key_rows), "dom", split_axis=0, concat_axis=0, tiled=True),
        lax.all_to_all(pack_rows(value_rows), "dom", split_axis=0, concat_axis=0, tiled=True),
        lax.all_to_all(arrival, "dom", split_axis=0, concat_axis=0, tiled=True),
    )
    slot_index = arrived.astype(jnp.int32)
    new_keys = place_rows(moved_keys, slot_index)
    new_values = place_rows(moved_values, slot_index)
    return (attn_out, new_keys, new_values, out_logw)


def solution(mesh):
    return jax.shard_map(
        local,
        mesh=mesh,
        in_specs=(
            P(None, "dom", "tp"),
            P(),
            P(None, "tp"),
            P(None, "tp"),
            P(None, "tp"),
            P("tp", None),
            P("dom", None, "tp"),
            P("dom", None, "tp"),
            P(None, "dom"),
            P(),
            P("tp"),
            P("dom"),
            P("dom"),
        ),
        out_specs=(P(None, "dom", "tp"), P("dom", None, "tp"), P("dom", None, "tp"), P("dom")),
        check_vma=False,
    )
```

profile of v0, /device:TPU:0, one launch (start us, length us, event | category | flops | bytes accessed | tf_op | source)
XLA Modules:
  0.0 234.3 jit_solution(9963035594114682076)
XLA Ops:
  8.2 1.3 fusion.34
  10.8 1.4 dynamic-update-slice
  12.2 9.5 %all-reduce = s32[8]{0:T(128)S(1)} all-reduce(s32[8]{0:T(128)S(1)} %dynamic-update-slice), channel_id=1, replica_groups=mesh['dom'=8,'tp'=4] {'dom'}, use_global_device_ids=true, to_apply=%add | all-reduce | flops 8 | bytes 64
  22.9 10.4 %all-to-all-start = ((bf16[8,8,1]{1,2,0:T(2,128)(2,1)}), bf16[8,8,1]{1,2,0:T(2,128)(2,1)S(1)}, u32[]{:S(2)}, u32[]{:S(2)}) async-start(bf16[8,8,1]{1,2,0:T(2,128)(2,1)} %fusion.23), calls=%async_computation.1 | async-start | bytes 8192 | tf_op jit(solution)/shard_map/all_to_all | solution.py:150
  34.0 16.7 %all_gather.9 = bf16[4,16,4096]{2,1,0:T(8,128)(2,1)S(1)} all-gather(bf16[4,16,1024]{2,1,0:T(8,128)(2,1)} %param.15), channel_id=1, replica_groups=mesh['dom'=8,'tp'=4] {'tp'}, dimensions={2}, use_global_device_ids=true | all-gather | bytes 655360 | tf_op jit(solution)/shard_map/all_gather | solution.py:84
  50.9 4.1 %copy.75 = bf16[256,4096]{1,0:T(8,128)(2,1)} copy(bf16[256,4096]{0,1:T(8,128)(2,1)} %bitcast.59) | data formatting | bytes 4194304 | tf_op jit(solution)/shard_map/dot_general | solution.py:95
  55.3 2.5 %fusion.15 = f32[4,16,2,128]{3,1,2,0:T(8,128)S(1)} fusion(bf16[2,128,4096,1]{2,1,0,3:T(8,128)(2,1)} %bitcast.60, bf16[4,16,4096]{2,1,0:T(8,128)(2,1)S(1)} %fusion.12), kind=kOutput, calls=%fused_computation.29 | convolution fusion | flops 134217728 | bytes 2686976 | tf_op jit(solution)/shard_map/dot_general | solution.py:95
  59.8 2.9 %gather_fusion = bf16[64,132,256]{2,1,0:T(8,128)(2,1)} fusion(bf16[16,132,256]{2,1,0:T(8,128)(2,1)S(1)} %pad_maximum_fusion.1, s32[1024]{0:T(1024)S(1)} %pad_clamp_fusion.1), kind=kCustom, calls=%fused_computation | custom fusion | bytes 8651008 | tf_op jit(solution)/shard_map/gather | solution.py:78
  62.7 2.9 %gather_fusion.1 = bf16[64,132,256]{2,1,0:T(8,128)(2,1)} fusion(bf16[16,132,256]{2,1,0:T(8,128)(2,1)S(1)} %pad_maximum_fusion, s32[1024]{0:T(1024)S(1)} %pad_clamp_fusion.1), kind=kCustom, calls=%fused_computation.1 | custom fusion | bytes 8651008 | tf_op jit(solution)/shard_map/gather | solution.py:78
  65.6 7.6 %broadcast_select_fusion = (bf16[64,132,256]{2,1,0:T(8,128)(2,1)}, bf16[64,132,256]{2,1,0:T(8,128)(2,1)}) fusion(bf16[64,132,256]{2,1,0:T(8,128)(2,1)} %gather_fusion.1, pred[64]{0:T(512)(128)(4,1)S(1)} %broadcast_compare_fusion, bf16[64,132,256]{2,1,0:T(8,128)(2,1)} %gather_fusion), kind=kLoop, calls=%fused_computation.8 | loop fusion | flops 4325376 | bytes 17301568 | tf_op jit(solution)/shard_map/jit(_where)/select_n | solution.py:78
  73.2 4.6 %all-to-all-start.1 = ((bf16[64,132,256]{2,1,0:T(8,128)(2,1)}), bf16[64,132,256]{2,1,0:T(8,128)(2,1)}, u32[]{:S(2)}, u32[]{:S(2)}) async-start(bf16[64,132,256]{2,1,0:T(8,128)(2,1)} %get-tuple-element.62), calls=%async_computation.2 | async-start | bytes 8912896 | tf_op jit(solution)/shard_map/all_to_all | solution.py:148
  79.4 11.3 %copy.81 = bf16[1024,4096]{1,0:T(8,128)(2,1)} copy(bf16[1024,4096]{0,1:T(8,128)(2,1)} %bitcast.57) | data formatting | bytes 16777216 | tf_op jit(solution)/shard_map/dot_general | solution.py:91
  90.7 6.1 %fusion.13 = f32[4,16,8,128]{3,1,2,0:T(8,128)S(1)} fusion(bf16[8,128,4096,1]{2,1,0,3:T(8,128)(2,1)} %bitcast.58, bf16[4,16,4096]{2,1,0:T(8,128)(2,1)S(1)} %copy-done.4), kind=kOutput, calls=%fused_computation.27 | convolution fusion | flops 536870912 | bytes 9175040 | tf_op jit(solution)/shard_map/dot_general | solution.py:91
  97.2 1.8 fusion.35
  99.0 30.7 %all-to-all-done.1 = bf16[64,132,256]{2,1,0:T(8,128)(2,1)} async-done(((bf16[64,132,256]{2,1,0:T(8,128)(2,1)}), bf16[64,132,256]{2,1,0:T(8,128)(2,1)}, u32[]{:S(2)}, u32[]{:S(2)}) %all-to-all-start.1) | async-done | bytes 4325408 | tf_op jit(solution)/shard_map/all_to_all | solution.py:148
  129.8 4.7 %all-to-all-start.2 = ((bf16[64,132,256]{2,1,0:T(8,128)(2,1)}), bf16[64,132,256]{2,1,0:T(8,128)(2,1)}, u32[]{:S(2)}, u32[]{:S(2)}) async-start(bf16[64,132,256]{2,1,0:T(8,128)(2,1)} %get-tuple-element.61), calls=%async_computation.3 | async-start | bytes 8912896 | tf_op jit(solution)/shard_map/all_to_all | solution.py:149
  135.1 6.0 %fusion.1 = f32[4,16,4096]{2,1,0:T(8,128)} fusion(bf16[4,16,1024]{2,1,0:T(8,128)(2,1)S(1)} %dot_general.37, bf16[1024,4096]{1,0:T(8,128)(2,1)} %param.20), kind=kOutput, calls=%fused_computation.6 | convolution fusion | flops 536870912 | bytes 9568256 | tf_op jit(solution)/shard_map/dot_general | solution.py:132
  142.3 27.8 %reduce-scatter.2.cloned.1.call-done = f32[4,16,1024]{2,1,0:T(8,128)} async-done(((f32[4,16,4096]{2,1,0:T(8,128)}), f32[4,16,1024]{2,1,0:T(8,128)}) %reduce-scatter.2.cloned.1.call-update) | async-done | bytes 262160 | tf_op jit(solution)/shard_map/reduce_scatter | solution.py:135
  170.1 1.8 multiply_reduce_fusion
  171.9 9.2 %all-reduce.1 = (f32[4,16]{1,0:T(4,128)S(1)}, f32[4,16]{1,0:T(4,128)S(1)}) all-reduce(f32[4,16]{1,0:T(4,128)S(1)} %get-tuple-element.41, f32[4,16]{1,0:T(4,128)S(1)} %get-tuple-element.40), channel_id=1, replica_groups=mesh['dom'=8,'tp'=4] {'tp'}, use_global_device_ids=true, to_apply=%region_12.13 | all-reduce | flops 128 | bytes 1024 | tf_op jit(solution)/shard_map/psum | solution.py:138
  181.7 12.4 %pmax.7 = f32[]{:T(128)} all-reduce(f32[]{:T(128)} %get-tuple-element.52), channel_id=1, replica_groups=mesh['dom'=8,'tp'=4] {'dom'}, use_global_device_ids=true, to_apply=%region_17.18 | all-reduce | flops 1 | bytes 8 | tf_op jit(solution)/shard_map/pmax | solution.py:144
  195.4 12.5 %psum.23 = f32[]{:T(128)} all-reduce(f32[]{:T(128)} %exponential_reduce_fusion), channel_id=1, replica_groups=mesh['dom'=8,'tp'=4] {'dom'}, use_global_device_ids=true, to_apply=%region_19.20 | all-reduce | flops 1 | bytes 8 | tf_op jit(solution)/shard_map/psum | solution.py:145
  209.8 7.6 %scatter_fusion = bf16[16,132,256]{2,1,0:T(8,128)(2,1)S(1)} fusion(bf16[16,132,256]{2,1,0:T(8,128)(2,1)S(1)} %broadcast.504.clone, s32[64]{0:T(128)S(1)} %fusion.29, bf16[64,132,256]{2,1,0:T(8,128)(2,1)} %all-to-all-done.1), kind=kCustom, calls=%fused_computation.3 | custom fusion | bytes 12976384 | tf_op jit(solution)/shard_map/scatter | solution.py:82
  218.7 7.6 %scatter_fusion.1 = bf16[16,132,256]{2,1,0:T(8,128)(2,1)S(1)} fusion(bf16[16,132,256]{2,1,0:T(8,128)(2,1)S(1)} %broadcast.504.clone.1, s32[64]{0:T(128)S(1)} %fusion.29, bf16[64,132,256]{2,1,0:T(8,128)(2,1)} %all-to-all-done.2), kind=kCustom, calls=%fused_computation.4 | custom fusion | bytes 12976384 | tf_op jit(solution)/shard_map/scatter | solution.py:82
  (84 shorter events, 15.1 us)
Async XLA Ops:
  7.2 51.0 %copy-start = (bf16[4096,256]{1,0:T(8,128)(2,1)S(1)}, bf16[4096,256]{1,0:T(8,128)(2,1)}, u32[]{:S(2)}) copy-start(bf16[4096,256]{1,0:T(8,128)(2,1)} %param.19) | copy-start | bytes 6291460
  22.9 50.3 %all-to-all-start = ((bf16[8,8,1]{1,2,0:T(2,128)(2,1)}), bf16[8,8,1]{1,2,0:T(2,128)(2,1)S(1)}, u32[]{:S(2)}, u32[]{:S(2)}) async-start(bf16[8,8,1]{1,2,0:T(2,128)(2,1)} %fusion.23), calls=%async_computation.1 | async-start | bytes 8192 | tf_op jit(solution)/shard_map/all_to_all | solution.py:150
  50.9 4.2 %copy-start.9 = (f32[4096]{0:T(1024)S(1)}, f32[4096]{0:T(1024)}, u32[]{:S(2)}) copy-start(f32[4096]{0:T(1024)} %param.16) | copy-start | bytes 49156
  55.3 2.9 %copy-start.3 = (bf16[4,16,4096]{2,1,0:T(8,128)(2,1)}, bf16[4,16,4096]{2,1,0:T(8,128)(2,1)S(1)}, u32[]{:S(2)}) copy-start(bf16[4,16,4096]{2,1,0:T(8,128)(2,1)S(1)} %fusion.12) | copy-start | bytes 1572868
  58.2 1.2 copy-start.6
  58.2 1.5 copy-start.7
  73.2 56.5 %all-to-all-start.1 = ((bf16[64,132,256]{2,1,0:T(8,128)(2,1)}), bf16[64,132,256]{2,1,0:T(8,128)(2,1)}, u32[]{:S(2)}, u32[]{:S(2)}) async-start(bf16[64,132,256]{2,1,0:T(8,128)(2,1)} %get-tuple-element.62), calls=%async_computation.2 | async-start | bytes 8912896 | tf_op jit(solution)/shard_map/all_to_all | solution.py:148
  79.4 11.3 %copy-start.4 = (bf16[4,16,4096]{2,1,0:T(8,128)(2,1)S(1)}, bf16[4,16,4096]{2,1,0:T(8,128)(2,1)}, u32[]{:S(2)}) copy-start(bf16[4,16,4096]{2,1,0:T(8,128)(2,1)} %copy-done.3) | copy-start | bytes 1572868
  90.7 6.5 %copy-start.5 = (bf16[16,132,2,128]{3,2,1,0:T(2,128)(2,1)S(1)}, bf16[16,132,2,128]{3,2,1,0:T(2,128)(2,1)}, u32[]{:S(2)}) copy-start(bf16[16,132,2,128]{3,2,1,0:T(2,128)(2,1)} %reshape.513) | copy-start | bytes 3244036
  129.8 4.7 %copy-start.13 = (f32[4,16,2,4,132]{4,3,0,2,1:T(4,128)S(1)}, f32[4,16,2,4,132]{4,3,0,2,1:T(4,128)}, u32[]{:S(2)}) copy-start(f32[4,16,2,4,132]{4,3,0,2,1:T(4,128)} %get-tuple-element.66) | copy-start | bytes 811012
  129.8 88.8 %all-to-all-start.2 = ((bf16[64,132,256]{2,1,0:T(8,128)(2,1)}), bf16[64,132,256]{2,1,0:T(8,128)(2,1)}, u32[]{:S(2)}, u32[]{:S(2)}) async-start(bf16[64,132,256]{2,1,0:T(8,128)(2,1)} %get-tuple-element.61), calls=%async_computation.3 | async-start | bytes 8912896 | tf_op jit(solution)/shard_map/all_to_all | solution.py:149
  134.5 35.6 %reduce-scatter.2.cloned.1.call-start = ((), (), s32[]{:S(2)}) async-start(), calls=%async_computation.4 | async-start | bytes 1310720 | tf_op jit(solution)/shard_map/reduce_scatter | solution.py:135
  135.1 6.0 %copy-start.11 = (s32[4,16]{1,0:T(4,128)S(1)}, s32[4,16]{1,0:T(4,128)}, u32[]{:S(2)}) copy-start(s32[4,16]{1,0:T(4,128)} %param.23) | copy-start | bytes 772
  135.1 6.1 %copy-start.2 = (bf16[128256]{0:T(1024)(128)(2,1)S(1)}, bf16[128256]{0:T(1024)(128)(2,1)}, u32[]{:S(2)}) copy-start(bf16[128256]{0:T(1024)(128)(2,1)} %param.24) | copy-start | bytes 769540
  141.1 29.0 %copy-start.8 = (bf16[4,16,1024]{2,1,0:T(8,128)(2,1)S(1)}, bf16[4,16,1024]{2,1,0:T(8,128)(2,1)}, u32[]{:S(2)}) copy-start(bf16[4,16,1024]{2,1,0:T(8,128)(2,1)} %param.15) | copy-start | bytes 393220
  141.1 29.0 %copy-start.10 = (f32[1024]{0:T(1024)S(1)}, f32[1024]{0:T(1024)}, u32[]{:S(2)}) copy-start(f32[1024]{0:T(1024)} %param.25) | copy-start | bytes 12292
  141.1 40.0 %copy-start.12 = (f32[16]{0:T(128)S(1)}, f32[16]{0:T(128)}, u32[]{:S(2)}) copy-start(f32[16]{0:T(128)} %param.26) | copy-start | bytes 196
  218.6 8.8 %copy-start.1 = (bf16[4096,256]{1,0:T(8,128)(2,1)S(1)}, bf16[4096,256]{1,0:T(8,128)(2,1)}, u32[]{:S(2)}) copy-start(bf16[4096,256]{1,0:T(8,128)(2,1)} %param.19) | copy-start | bytes 6291460
Sparse Core Ops, SparseCore 0:
  141.3 28.7 reduce-scatter.1
where the time goes:
time: 236 us; the launch traced here: 234 us
  blocking collectives  60.3 us (26%)
  waiting for transfers between devices  58.6 us (25%)
  local copies, waits for them, and re-layouts  46.2 us (20%)
  starting transfers between devices  19.8 us (8%)
  matrix products  17.4 us (7%)
  other arithmetic  16.4 us (7%)
  between operations  15.7 us (7%)
    all_to_all x1, waiting for transfers between devices, local(): lax.all_to_all(pack_rows(key_rows), 'dom', split_axis=0, concat_axis=0, t...  30.7 us
    reduce_scatter x1, waiting for transfers between devices, local(): lax.psum_scatter(partial_value, 'tp', scatter_dimension=2, tiled=True)  27.8 us
    all_gather x1, blocking collectives, local(): gathered = lax.all_gather(activations, 'tp', axis=2, tiled=True)  16.7 us
    scatter x2, local copies, waits for them, and re-layouts, place_rows(): return blank.at[slot_index].set(tensor, mode='drop')  15.2 us
    psum x1, blocking collectives, local(): lax.psum(jnp.sum(jnp.exp(particle_log_weight - largest)), 'dom')  12.5 us
    pmax x1, blocking collectives, local(): largest = lax.pmax(jnp.max(particle_log_weight), 'dom')  12.4 us
    dot_general x1, local copies, waits for them, and re-layouts, local(): jnp.dot(flat_rows, w_query, preferred_element_type=jnp.float32)  11.3 us
    all_to_all x1, starting transfers between devices, local(): lax.all_to_all(arrival, 'dom', split_axis=0, concat_axis=0, tiled=True)  10.4 us
  transfers between devices with their start and end apart: 4, of which 2 were waited for; matrix products, arithmetic and copies ran while one was open for 27% of the time, Pallas kernels for 0%

commit v1 on v0

--- a/solution.py
+++ b/solution.py
@@ -61,25 +61,12 @@
     kv_local = w_key.shape[1] // HD
     q_local = w_query.shape[1] // HD
     group_size = q_local // kv_local
-    capacity = 4 * particle_count // dom_size
-    total_copies = jnp.sum(copy_counts)
-    offset = entering(total_copies, "dom", add_counts, jnp.int32(0))
-    starts = jnp.cumsum(copy_counts) - copy_counts
-    position = jnp.arange(dom_size * capacity, dtype=jnp.int32)
-    target = position // capacity
-    copy_rank = position % capacity * dom_size + (target - offset) % dom_size
-    is_live = copy_rank < total_copies
-    source = jnp.sum((starts[None, :] <= copy_rank[:, None]).astype(jnp.int32), 1) - 1
-    arrival = jnp.where(is_live, (offset + copy_rank) // dom_size, particle_count).astype(
-        jnp.bfloat16
-    )
-
-    def pack_rows(tensor):
-        return jnp.where(is_live[:, None, None], tensor[source], jnp.zeros((), tensor.dtype))
-
-    def place_rows(tensor, slot_index):
-        blank = jnp.zeros((particle_count,) + tensor.shape[1:], tensor.dtype)
-        return blank.at[slot_index].set(tensor, mode="drop")
+    all_counts = lax.all_gather(copy_counts, "dom", axis=0, tiled=True)
+    copy_ends = jnp.cumsum(all_counts)
+    ranks = jnp.arange(particle_count, dtype=jnp.int32) * dom_size + lax.axis_index("dom")
+    ancestor = jnp.sum((copy_ends[None, :] <= ranks[:, None]).astype(jnp.int32), 1)
+    all_keys = lax.all_gather(cache_keys, "dom", axis=0, tiled=True)
+    all_values = lax.all_gather(cache_values, "dom", axis=0, tiled=True)
 
     gathered = lax.all_gather(activations, "tp", axis=2, tiled=True)
     inputs = gathered.astype(jnp.float32)
@@ -144,14 +131,12 @@
     largest = lax.pmax(jnp.max(particle_log_weight), "dom")
     mass_total = lax.psum(jnp.sum(jnp.exp(particle_log_weight - largest)), "dom")
     out_logw = particle_log_weight - (largest + jnp.log(mass_total))
-    moved_keys, moved_values, arrived = (
-        lax.all_to_all(pack_rows(key_rows), "dom", split_axis=0, concat_axis=0, tiled=True),
-        lax.all_to_all(pack_rows(value_rows), "dom", split_axis=0, concat_axis=0, tiled=True),
-        lax.all_to_all(arrival, "dom", split_axis=0, concat_axis=0, tiled=True),
-    )
-    slot_index = arrived.astype(jnp.int32)
-    new_keys = place_rows(moved_keys, slot_index)
-    new_values = place_rows(moved_values, slot_index)
+    fresh = lax.all_gather(
+        jnp.concatenate([fresh_keys, fresh_values], 2), "dom", axis=0, tiled=True
+    )[ancestor]
+    width = fresh_keys.shape[2]
+    new_keys = jnp.concatenate([all_keys[ancestor], fresh[..., :width]], 1)
+    new_values = jnp.concatenate([all_values[ancestor], fresh[..., width:]], 1)
     return (attn_out, new_keys, new_values, out_logw)
 
 

time: 236 us -> 193 us (0.82)
  starting transfers between devices: 19.8 us -> 0.12 us
  local copies, waits for them, and re-layouts: 46.2 us -> 32.8 us
  blocking collectives: 60.3 us -> 72.5 us
  waiting for transfers between devices: 58.6 us -> 46.5 us
  other arithmetic: 16.4 us -> 5.85 us
    all_gather x0 -> x2, waiting for transfers between devices: none -> 40.9 us  [the longest x1 40.9 us: local(): all_values = lax.all_gather(cache_values, 'dom', axis=0, tiled=True)]
    all_to_all x3 -> x0, waiting for transfers between devices: 30.7 us -> none  [the longest x1 30.7 us: local(): lax.all_to_all(pack_rows(key_rows), 'dom', split_axis=0, concat_axis=0, t...]
    reduce_scatter x1, waiting for transfers between devices: 27.8 us -> 4.54 us  [local(): lax.psum_scatter(partial_value, 'tp', scatter_dimension=2, tiled=True)]
    all_to_all x3 -> x0, starting transfers between devices: 19.7 us -> none  [the longest x1 10.4 us: local(): lax.all_to_all(arrival, 'dom', split_axis=0, concat_axis=0, tiled=True)]
    scatter x2 -> x0, local copies, waits for them, and re-layouts: 15.2 us -> none  [place_rows(): return blank.at[slot_index].set(tensor, mode='drop')]
    all_gather x0 -> x1, blocking collectives: none -> 11.6 us  [local(): lax.all_gather(jnp.concatenate([fresh_keys, fresh_values], 2), 'dom', axi...]
    select_n x3 -> x1, other arithmetic: 7.66 us -> 0.01 us  [local(): new_keys = jnp.concatenate([all_keys[ancestor], fresh[..., :width]], 1)]
    gather x2 -> x3, local copies, waits for them, and re-layouts: 5.73 us -> 9.05 us  [the longest x1 4.45 us: local(): new_keys = jnp.concatenate([all_keys[ancestor], fresh[..., :width]], 1)]
  transfers between devices with their start and end apart: 4 -> 3, of which waited for: 2 -> 2; matrix products, arithmetic and copies ran while one was open for 27% -> 7% of each run, Pallas kernels for 0% -> 0%
where the time goes in v1:
time: 193 us; the launch traced here: 192 us
  blocking collectives  72.5 us (38%)
  waiting for transfers between devices  46.5 us (24%)
  local copies, waits for them, and re-layouts  32.8 us (17%)
  between operations  17.8 us (9%)
  matrix products  16.5 us (9%)
  other arithmetic  5.85 us (3%)
    all_gather x1, waiting for transfers between devices, local(): all_values = lax.all_gather(cache_values, 'dom', axis=0, tiled=True)  40.9 us
    all_gather x1, blocking collectives, local(): gathered = lax.all_gather(activations, 'tp', axis=2, tiled=True)  17.7 us
    pmax x1, blocking collectives, local(): largest = lax.pmax(jnp.max(particle_log_weight), 'dom')  13.4 us
    psum x1, blocking collectives, local(): lax.psum(jnp.sum(jnp.exp(particle_log_weight - largest)), 'dom')  12.6 us
    all_gather x1, blocking collectives, local(): lax.all_gather(jnp.concatenate([fresh_keys, fresh_values], 2), 'dom', axi...  11.6 us
    dot_general x1, local copies, waits for them, and re-layouts, local(): jnp.dot(flat_rows, w_query, preferred_element_type=jnp.float32)  11.3 us
    psum x1, blocking collectives, local(): lax.psum((jnp.sum(summed * twist_vec, -1), jnp.sum(summed * summed, -1)),...  9.23 us
    unnamed x1, blocking collectives  8.01 us
  transfers between devices with their start and end apart: 3, of which 2 were waited for; matrix products, arithmetic and copies ran while one was open for 7% of the time, Pallas kernels for 0%

profile of v1, /device:TPU:0, one launch (start us, length us, event | category | flops | bytes accessed | tf_op | source)
XLA Modules:
  0.0 192.2 jit_solution(1727747766520244316)
XLA Ops:
  8.1 17.7 %all_gather.15 = bf16[4,16,4096]{2,1,0:T(8,128)(2,1)S(1)} all-gather(bf16[4,16,1024]{2,1,0:T(8,128)(2,1)} %param.13), channel_id=1, replica_groups=mesh['dom'=8,'tp'=4] {'tp'}, dimensions={2}, use_global_device_ids=true | all-gather | bytes 655360 | tf_op jit(solution)/shard_map/all_gather | solution.py:71
  26.0 4.1 %copy.77 = bf16[256,4096]{1,0:T(8,128)(2,1)} copy(bf16[256,4096]{0,1:T(8,128)(2,1)} %bitcast.54) | data formatting | bytes 4194304 | tf_op jit(solution)/shard_map/dot_general | solution.py:82
  30.4 2.6 %fusion.15 = f32[4,16,2,128]{3,1,2,0:T(8,128)S(1)} fusion(bf16[2,128,4096,1]{2,1,0,3:T(8,128)(2,1)} %bitcast.55, bf16[4,16,4096]{2,1,0:T(8,128)(2,1)S(1)} %fusion.12), kind=kOutput, calls=%fused_computation.28 | convolution fusion | flops 134217728 | bytes 2686976 | tf_op jit(solution)/shard_map/dot_general | solution.py:82
  33.4 1.2 reshape.223
  34.5 11.3 %copy.82 = bf16[1024,4096]{1,0:T(8,128)(2,1)} copy(bf16[1024,4096]{0,1:T(8,128)(2,1)} %bitcast.52) | data formatting | bytes 16777216 | tf_op jit(solution)/shard_map/dot_general | solution.py:78
  45.9 6.0 %fusion.13 = f32[4,16,8,128]{3,1,2,0:T(8,128)S(1)} fusion(bf16[8,128,4096,1]{2,1,0,3:T(8,128)(2,1)} %bitcast.53, bf16[4,16,4096]{2,1,0:T(8,128)(2,1)S(1)} %copy-done.6), kind=kOutput, calls=%fused_computation.26 | convolution fusion | flops 536870912 | bytes 9175040 | tf_op jit(solution)/shard_map/dot_general | solution.py:78
  53.2 1.2 reshape.222
  54.4 1.1 fusion.26
  56.2 5.9 %fusion.1 = f32[4,16,4096]{2,1,0:T(8,128)} fusion(bf16[4,16,1024]{2,1,0:T(8,128)(2,1)S(1)} %dot_general.37, bf16[1024,4096]{1,0:T(8,128)(2,1)} %param.18), kind=kOutput, calls=%fused_computation.5 | convolution fusion | flops 536870912 | bytes 9568256 | tf_op jit(solution)/shard_map/dot_general | solution.py:119
  63.5 0.8 gather_fusion.3
  66.0 8.0 %all-reduce = s32[128]{0:T(128)S(1)} all-reduce(s32[128]{0:T(128)S(1)} %dynamic-update-slice), channel_id=1, replica_groups=mesh['dom'=8,'tp'=4] {'dom'}, use_global_device_ids=true, to_apply=%add | all-reduce | flops 128 | bytes 1024
  74.6 11.6 %all_gather.18 = bf16[128,4,512]{2,1,0:T(4,128)(2,1)S(1)} all-gather(bf16[16,4,512]{2,1,0:T(4,128)(2,1)S(1)} %copy.67), channel_id=1, replica_groups=mesh['dom'=8,'tp'=4] {'dom'}, dimensions={0}, use_global_device_ids=true | all-gather | bytes 589824 | tf_op jit(solution)/shard_map/all_gather | solution.py:134
  86.9 4.5 %reduce-scatter.2.cloned.1.call-done = f32[4,16,1024]{2,1,0:T(8,128)} async-done(((f32[4,16,4096]{2,1,0:T(8,128)}), f32[4,16,1024]{2,1,0:T(8,128)}) %reduce-scatter.2.cloned.1.call-update) | async-done | bytes 262160 | tf_op jit(solution)/shard_map/reduce_scatter | solution.py:122
  91.4 1.7 multiply_reduce_fusion
  93.2 9.2 %all-reduce.1 = (f32[4,16]{1,0:T(4,128)S(1)}, f32[4,16]{1,0:T(4,128)S(1)}) all-reduce(f32[4,16]{1,0:T(4,128)S(1)} %get-tuple-element.17, f32[4,16]{1,0:T(4,128)S(1)} %get-tuple-element.16), channel_id=1, replica_groups=mesh['dom'=8,'tp'=4] {'tp'}, use_global_device_ids=true, to_apply=%region_7.8 | all-reduce | flops 128 | bytes 1024 | tf_op jit(solution)/shard_map/psum | solution.py:125
  103.0 13.4 %pmax.7 = f32[]{:T(128)} all-reduce(f32[]{:T(128)} %get-tuple-element.20), channel_id=1, replica_groups=mesh['dom'=8,'tp'=4] {'dom'}, use_global_device_ids=true, to_apply=%region_12.13 | all-reduce | flops 1 | bytes 8 | tf_op jit(solution)/shard_map/pmax | solution.py:131
  116.4 1.2 exponential_reduce_fusion
  117.7 12.6 %psum.23 = f32[]{:T(128)} all-reduce(f32[]{:T(128)} %exponential_reduce_fusion), channel_id=1, replica_groups=mesh['dom'=8,'tp'=4] {'dom'}, use_global_device_ids=true, to_apply=%region_14.15 | all-reduce | flops 1 | bytes 8 | tf_op jit(solution)/shard_map/psum | solution.py:132
  132.1 4.4 %gather_fusion = bf16[16,128,256]{2,1,0:T(8,128)(2,1)S(1)} fusion(bf16[128,128,256]{2,1,0:T(8,128)(2,1)} %all-gather.3.cloned.1.call-done, s32[1024]{0:T(1024)S(1)} %pad_clamp_fusion.1), kind=kCustom, calls=%fused_computation | custom fusion | bytes 2097216 | tf_op jit(solution)/shard_map/gather | solution.py:138
  136.6 1.2 copy.68
  137.8 40.9 %all-gather.5.cloned.1.call-done = bf16[128,128,256]{2,1,0:T(8,128)(2,1)} async-done(((bf16[16,128,256]{2,1,0:T(8,128)(2,1)}), bf16[128,128,256]{2,1,0:T(8,128)(2,1)}) %all-gather.5.cloned.1.call-update) | async-done | bytes 8388624 | tf_op jit(solution)/shard_map/all_gather | solution.py:69
  178.7 4.0 %gather_fusion.2 = bf16[16,128,256]{2,1,0:T(8,128)(2,1)S(1)} fusion(bf16[128,128,256]{2,1,0:T(8,128)(2,1)} %all-gather.5.cloned.1.call-done, s32[1024]{0:T(1024)S(1)} %pad_clamp_fusion.1), kind=kCustom, calls=%fused_computation.2 | custom fusion | bytes 2097216 | tf_op jit(solution)/shard_map/gather | solution.py:139
  182.8 1.2 copy.69
  184.0 0.7 copy-done.1
  (82 shorter events, 7.7 us)
Async XLA Ops:
  8.0 44.3 %copy-start = (bf16[4096,256]{1,0:T(8,128)(2,1)S(1)}, bf16[4096,256]{1,0:T(8,128)(2,1)}, u32[]{:S(2)}) copy-start(bf16[4096,256]{1,0:T(8,128)(2,1)} %param.17) | copy-start | bytes 6291460
  8.0 83.4 %reduce-scatter.2.cloned.1.call-start = ((), (), s32[]{:S(2)}) async-start(), calls=%async_computation.1 | async-start | bytes 1310720 | tf_op jit(solution)/shard_map/reduce_scatter | solution.py:122
  26.0 4.2 %copy-start.10 = (f32[4096]{0:T(1024)S(1)}, f32[4096]{0:T(1024)}, u32[]{:S(2)}) copy-start(f32[4096]{0:T(1024)} %param.14) | copy-start | bytes 49156
  30.3 2.9 %copy-start.5 = (bf16[4,16,4096]{2,1,0:T(8,128)(2,1)}, bf16[4,16,4096]{2,1,0:T(8,128)(2,1)S(1)}, u32[]{:S(2)}) copy-start(bf16[4,16,4096]{2,1,0:T(8,128)(2,1)S(1)} %fusion.12) | copy-start | bytes 1572868
  30.4 2.9 %copy-start.3 = (bf16[16,128,256]{2,1,0:T(8,128)(2,1)S(1)}, bf16[16,128,256]{2,1,0:T(8,128)(2,1)}, u32[]{:S(2)}) copy-start(bf16[16,128,256]{2,1,0:T(8,128)(2,1)} %param.19) | copy-start | bytes 3145732
  34.5 11.3 %copy-start.6 = (bf16[4,16,4096]{2,1,0:T(8,128)(2,1)S(1)}, bf16[4,16,4096]{2,1,0:T(8,128)(2,1)}, u32[]{:S(2)}) copy-start(bf16[4,16,4096]{2,1,0:T(8,128)(2,1)} %copy-done.5) | copy-start | bytes 1572868
  51.9 1.2 copy-start.4
  53.1 1.3 copy-start.7
  54.4 1.2 copy-start.8
  62.2 1.3 copy-start.12
  62.2 1.4 copy-start.2
  62.2 2.3 %copy-start.15 = (u32[32]{0:T(128)S(1)}, u32[32]{0:T(128)}, u32[]{:S(2)}) copy-start(u32[32]{0:T(128)} %constant.45) | copy-start | bytes 388
  62.2 3.6 %copy-start.14 = (s32[16]{0:T(128)S(1)}, s32[16]{0:T(128)}, u32[]{:S(2)}) copy-start(s32[16]{0:T(128)} %param.25) | copy-start | bytes 196
  62.2 29.2 %copy-start.9 = (bf16[4,16,1024]{2,1,0:T(8,128)(2,1)S(1)}, bf16[4,16,1024]{2,1,0:T(8,128)(2,1)}, u32[]{:S(2)}) copy-start(bf16[4,16,1024]{2,1,0:T(8,128)(2,1)} %param.13) | copy-start | bytes 393220
  62.2 29.2 %copy-start.11 = (f32[1024]{0:T(1024)S(1)}, f32[1024]{0:T(1024)}, u32[]{:S(2)}) copy-start(f32[1024]{0:T(1024)} %param.23) | copy-start | bytes 12292
  62.2 69.9 %all-gather.3.cloned.1.call-start = ((), (), s32[]{:S(2)}) async-start(), calls=%async_computation.2 | async-start | bytes 9437184 | tf_op jit(solution)/shard_map/all_gather | solution.py:68
  62.8 39.6 %copy-start.13 = (f32[16]{0:T(128)S(1)}, f32[16]{0:T(128)}, u32[]{:S(2)}) copy-start(f32[16]{0:T(128)} %param.24) | copy-start | bytes 196
  62.8 115.9 %all-gather.5.cloned.1.call-start = ((), (), s32[]{:S(2)}) async-start(), calls=%async_computation.3 | async-start | bytes 9437184 | tf_op jit(solution)/shard_map/all_gather | solution.py:69
  182.7 2.0 %copy-start.1 = (bf16[4096,256]{1,0:T(8,128)(2,1)S(1)}, bf16[4096,256]{1,0:T(8,128)(2,1)}, u32[]{:S(2)}) copy-start(bf16[4096,256]{1,0:T(8,128)(2,1)} %param.17) | copy-start | bytes 6291460
Sparse Core Ops, SparseCore 0:
  62.3 29.0 reduce-scatter.1
Sparse Core Ops, SparseCore 1:
  64.6 58.2 all-gather.2
  124.6 54.1 all-gather.4

commit v2 on v1

--- a/solution.py
+++ b/solution.py
@@ -1,21 +1,15 @@
+import functools
+
 import jax
 import jax.numpy as jnp
+import numpy as np
 from jax import lax
+from jax.experimental import pallas as pl
+from jax.experimental.pallas import tpu as pltpu
 from jax.sharding import PartitionSpec as P
 
 D = 4096
 HD = 128
-
-
-def entering(part, axis, combine, identity):
-    place = lax.axis_index(axis)
-    gathered = lax.all_gather(part, axis)
-    state = jnp.zeros_like(part) + jnp.asarray(identity, part.dtype)
-
-    def one(lap, state):
-        return combine(state, lax.dynamic_index_in_dim(gathered, lap, 0, False))
-
-    return lax.fori_loop(0, place, one, state)
 
 
 def rotate(tensor, positions):
@@ -33,10 +27,6 @@
         ],
         -1,
     )
-
-
-def add_counts(former, latter):
-    return former + latter
 
 
 def local(
@@ -140,9 +130,403 @@
     return (attn_out, new_keys, new_values, out_logw)
 
 
+MESH = pl.DeviceIdType.MESH
+
+
+def layer_kernel(
+    steps, parts, doms, tps,
+    act, gain, wq, wk, wv, wo, ck, cv, reward, twist, prev, counts, cosine, sine,
+    attn_out, all_k, all_v, fresh_sel, out_lw, anc_out,
+    act_all, wq_v, wk_v, wv_v, wo_v, ck_v, cv_v, qs, cx, sc1, ctx_b, fresh, fresh_all,
+    rs_send, rs_recv, sc_all, lw_all, cnt_all,
+    loc, tp_send, tp_recv, dom_send, dom_recv, blk_send, blk_recv,
+):
+    f32, bf16 = jnp.float32, jnp.bfloat16
+    me_d = lax.axis_index("dom")
+    me_t = lax.axis_index("tp")
+    rows, width = act.shape
+    half = parts // 2
+    kvw = wk.shape[1]
+    groups = kvw // HD
+    per = wq.shape[1] // kvw
+    pack = steps * per
+    c = me_d % 2
+    x = (me_d // 2) % 2
+    y = me_d // 4
+    sib = me_d + 1 - 2 * c
+    xn = me_d + 2 - 4 * x
+    yn = me_d + 4 - 8 * y
+    dn = xn + 4 - 8 * y
+
+    barrier = pltpu.get_barrier_semaphore()
+    for k in range(1, tps):
+        pl.semaphore_signal(
+            barrier, inc=1, device_id=(me_d, (me_t + k) % tps), device_id_type=MESH
+        )
+    for k in range(1, doms):
+        pl.semaphore_signal(
+            barrier, inc=1, device_id=((me_d + k) % doms, me_t), device_id_type=MESH
+        )
+
+    def fetch(i, src, dst):
+        copy = pltpu.make_async_copy(src, dst, loc.at[i])
+        copy.start()
+        return copy
+
+    own_act = fetch(0, act, act_all.at[me_t])
+    load_q = fetch(1, wq, wq_v)
+    load_k = fetch(2, wk, wk_v)
+    load_v = fetch(3, wv, wv_v)
+    load_ck = fetch(4, ck, ck_v)
+    load_cv = fetch(5, cv, cv_v)
+    load_o = fetch(6, wo, wo_v)
+
+    cnt_all[me_d] = jnp.broadcast_to(counts[...], cnt_all.shape[1:])
+    pl.semaphore_wait(barrier, tps + doms - 2)
+
+    def tp_push(base, k, src, dst):
+        copy = pltpu.make_async_remote_copy(
+            src_ref=src, dst_ref=dst, send_sem=tp_send.at[base + k - 1],
+            recv_sem=tp_recv.at[base + k - 1],
+            device_id=(me_d, (me_t + k) % tps), device_id_type=MESH,
+        )
+        copy.start()
+        return copy
+
+    def dom_push(base, k, src, dst):
+        copy = pltpu.make_async_remote_copy(
+            src_ref=src, dst_ref=dst, send_sem=dom_send.at[base + k - 1],
+            recv_sem=dom_recv.at[base + k - 1],
+            device_id=((me_d + k) % doms, me_t), device_id_type=MESH,
+        )
+        copy.start()
+        return copy
+
+    acts = [tp_push(0, k, act, act_all.at[me_t]) for k in range(1, tps)]
+
+    def piece(kind, to, which, h, slot, own):
+        dst = (all_k, all_v)[which].at[slot, pl.ds(h * half, half)]
+        src = (ck, cv)[which].at[pl.ds(h * half, half)] if own else dst
+        i = kind * 4 + h * 2 + which
+        copy = pltpu.make_async_remote_copy(
+            src_ref=src, dst_ref=dst, send_sem=blk_send.at[i], recv_sem=blk_recv.at[i],
+            device_id=(to, me_t), device_id_type=MESH,
+        )
+        copy.start()
+        return copy
+
+    moves = {}
+    for h, kind, to in ((0, 0, xn), (1, 1, yn), (1, 0, xn), (0, 1, yn)):
+        for which in range(2):
+            moves[kind, h, which] = piece(kind, to, which, h, me_d, True)
+    cnts = [dom_push(0, k, cnt_all.at[me_d], cnt_all.at[me_d]) for k in range(1, doms)]
+    for h in range(2):
+        for which in range(2):
+            moves[3, h, which] = piece(3, sib, which, h, me_d, True)
+
+    own_act.wait()
+    for copy in acts:
+        copy.wait()
+    square = jnp.zeros((rows, 1), f32)
+    for t in range(tps):
+        u = act_all[t].astype(f32)
+        square = square + jnp.sum(u * u, -1, keepdims=True)
+    inv = lax.rsqrt(square / (width * tps) + 1e-05)
+    normed = []
+    for t in range(tps):
+        u = act_all[t].astype(f32)
+        normed.append((u * inv * gain[:, t * width : (t + 1) * width]).astype(bf16))
+
+    def project(w):
+        total = None
+        for t in range(tps):
+            part = jnp.dot(
+                normed[t], w[t * width : (t + 1) * width, :], preferred_element_type=f32
+            )
+            total = part if total is None else total + part
+        return total
+
+    cos_t, sin_t = cosine[...], sine[...]
+
+    def turn(u):
+        return u * cos_t + pltpu.roll(u, HD // 2, 1) * sin_t
+
+    load_k.wait()
+    load_v.wait()
+    keys = project(wk_v)
+    for g in range(groups):
+        fresh[:, g * HD : (g + 1) * HD] = turn(keys[:, g * HD : (g + 1) * HD]).astype(bf16)
+    fresh[:, kvw:] = project(wv_v).astype(bf16)
+    fresh_all[me_d] = fresh[...]
+    news = [dom_push(doms - 1, k, fresh, fresh_all.at[me_d]) for k in range(1, doms)]
+    load_q.wait()
+    query = project(wq_v)
+    for h in range(groups * per):
+        g, j = h // per, h % per
+        turned = turn(query[:, h * HD : (h + 1) * HD])
+        for s in range(steps):
+            qs[g, :, s * per + j, :] = turned[s * parts : (s + 1) * parts]
+    load_ck.wait()
+    load_cv.wait()
+    put_k = fetch(7, ck_v, all_k.at[me_d])
+    put_v = fetch(8, cv_v, all_v.at[me_d])
+
+    lines = parts * pack
+    row = lax.broadcasted_iota(jnp.int32, (lines, rows), 0)
+    col = lax.broadcasted_iota(jnp.int32, (lines, rows), 1)
+    allowed = (row // pack == col % parts) & (col // parts <= (row % pack) // per)
+    scale = HD**0.5
+    for g in range(groups):
+        lanes = slice(g * HD, (g + 1) * HD)
+        qg = qs[g].reshape(lines, HD).astype(bf16)
+        for n in range(parts):
+            sc1[g, n * pack : (n + 1) * pack, :] = lax.dot_general(
+                qg[n * pack : (n + 1) * pack], ck_v[n, :, lanes],
+                (((1,), (1,)), ((), ())), preferred_element_type=f32,
+            )
+        near = lax.dot_general(
+            qg, fresh[:, lanes], (((1,), (1,)), ((), ())), preferred_element_type=f32
+        )
+        near = jnp.where(allowed, near / scale, -jnp.inf)
+        far = sc1[g] / scale
+        top = jnp.maximum(
+            jnp.max(far, -1, keepdims=True), jnp.max(near, -1, keepdims=True)
+        )
+        far = jnp.exp(far - top)
+        near = jnp.exp(near - top)
+        mass = jnp.sum(far, -1, keepdims=True) + jnp.sum(near, -1, keepdims=True)
+        far = (far / mass).astype(bf16)
+        near = (near / mass).astype(bf16)
+        extra = jnp.dot(
+            near, fresh[:, kvw + g * HD : kvw + (g + 1) * HD], preferred_element_type=f32
+        )
+        for n in range(parts):
+            span = slice(n * pack, (n + 1) * pack)
+            cx[g, n] = extra[span] + jnp.dot(
+                far[span], cv_v[n, :, lanes], preferred_element_type=f32
+            )
+    for h in range(groups * per):
+        g, j = h // per, h % per
+        for s in range(steps):
+            ctx_b[s * parts : (s + 1) * parts, h * HD : (h + 1) * HD] = cx[
+                g, :, s * per + j, :
+            ].astype(bf16)
+    load_o.wait()
+
+    def mix(p):
+        return jnp.dot(
+            ctx_b[...], wo_v[:, pl.ds(pl.multiple_of(p * width, HD), width)],
+            preferred_element_type=f32,
+        )
+
+    sums = []
+    for k in range(1, tps):
+        rs_send[k - 1] = mix((me_t + k) % tps)
+        sums.append(tp_push(tps - 1, k, rs_send.at[k - 1], rs_recv.at[k - 1]))
+    head = mix(me_t)
+    for k in range(1, tps):
+        sums[k - 1].wait()
+        head = head + rs_recv[k - 1]
+    attn_out[...] = head.astype(bf16)
+    summed = act_all[me_t].astype(f32) + head
+    along = jnp.sum(summed * twist[...], -1, keepdims=True)
+    energy = jnp.sum(summed * summed, -1, keepdims=True)
+    lane = lax.broadcasted_iota(jnp.int32, (rows, HD), 1)
+    sc_all[me_t] = jnp.where(lane < HD // 2, along, energy)
+    scores = [
+        tp_push(2 * (tps - 1), k, sc_all.at[me_t], sc_all.at[me_t]) for k in range(1, tps)
+    ]
+    for copy in scores:
+        copy.wait()
+    both = sc_all[0]
+    for t in range(1, tps):
+        both = both + sc_all[t]
+    score = reward[...] + both[:, :1] / jnp.sqrt(both[:, HD - 1 :] / (width * tps) + 1e-06)
+    total = score[:parts]
+    for s in range(1, steps):
+        total = total + score[s * parts : (s + 1) * parts]
+    mine = jnp.broadcast_to(prev[...] + total, (parts, HD))
+    lw_all[me_d] = mine
+    lws = [
+        dom_push(2 * (doms - 1), k, lw_all.at[me_d], lw_all.at[me_d]) for k in range(1, doms)
+    ]
+
+    def done(kind, h):
+        for which in range(2):
+            moves[kind, h, which].wait_recv()
+
+    def relay(kind, to, h, slot):
+        for which in range(2):
+            moves[kind, h, which] = piece(kind, to, which, h, slot, False)
+
+    done(0, 0)
+    relay(2, yn, 0, xn)
+    relay(4, sib, 0, xn)
+    done(1, 1)
+    relay(6, xn, 1, yn)
+    relay(5, sib, 1, yn)
+    done(0, 1)
+    relay(4, sib, 1, xn)
+    done(1, 0)
+    relay(5, sib, 0, yn)
+
+    for copy in cnts:
+        copy.wait()
+    for copy in news:
+        copy.wait()
+    whole = parts * doms
+    number = cnt_all[...].reshape(whole, HD).astype(bf16)
+    lower = lax.broadcasted_iota(jnp.int32, (whole, whole), 0)
+    upper = lax.broadcasted_iota(jnp.int32, (whole, whole), 1)
+    ends = jnp.dot(
+        (upper <= lower).astype(f32).astype(bf16), number, preferred_element_type=f32
+    )
+    slot = lax.broadcasted_iota(jnp.int32, (whole, HD), 1)
+
+    def ancestor(place):
+        rank = (place * doms + me_d).astype(f32)
+        return jnp.sum((ends <= rank).astype(f32), 0, keepdims=True).astype(jnp.int32)
+
+    anc_out[...] = jnp.broadcast_to(ancestor(slot), anc_out.shape)
+    lanes = lax.broadcasted_iota(jnp.int32, (1, HD), 1)
+    wide = ancestor(slot // 8)
+    target = (wide // parts) * rows + (lanes % 8) * parts + wide % parts
+    target = jnp.where(lanes % 8 < steps, target, -1)
+    index = lax.broadcasted_iota(jnp.int32, (doms * rows, HD), 0)
+    pick = (index == target).astype(f32).astype(bf16)
+    fresh_sel[...] = lax.dot_general(
+        pick, fresh_all[...].reshape(doms * rows, 2 * kvw),
+        (((0,), (0,)), ((), ())), preferred_element_type=f32,
+    ).astype(bf16)
+
+    for copy in lws:
+        copy.wait()
+    largest = jnp.max(lw_all[...], (0, 1), keepdims=True)[0]
+    mass = jnp.sum(jnp.exp(lw_all[...] - largest[None]), (0, 1), keepdims=True)[0]
+    out_lw[...] = mine - (largest + jnp.log(mass))
+
+    done(2, 0)
+    relay_d0 = [piece(7, sib, which, 0, dn, False) for which in range(2)]
+    done(6, 1)
+    relay_d1 = [piece(7, sib, which, 1, dn, False) for which in range(2)]
+    for kind in (3, 4, 5):
+        for h in range(2):
+            done(kind, h)
+    for copy in moves.values():
+        copy.wait_send()
+    for copy in relay_d0 + relay_d1:
+        copy.wait()
+    put_k.wait()
+    put_v.wait()
+
+
+def select_kernel(parts, steps, anc, fresh_sel, all_k, all_v, new_k, new_v, sem):
+    span = all_k.shape[2]
+    width = all_k.shape[3]
+    copies = []
+    for i in range(parts):
+        a = anc[i]
+        d, n = a // parts, a % parts
+        for which, (src, dst) in enumerate(((all_k, new_k), (all_v, new_v))):
+            copy = pltpu.make_async_copy(
+                src.at[d, n], dst.at[i, pl.ds(0, span)], sem.at[2 * i + which]
+            )
+            copy.start()
+            copies.append(copy)
+    for i in range(parts):
+        new_k[i, span:, :] = fresh_sel[i * 8 : i * 8 + steps, :width]
+        new_v[i, span:, :] = fresh_sel[i * 8 : i * 8 + steps, width:]
+    for copy in copies:
+        copy.wait()
+
+
+def fused(
+    activations, norm_gain, w_query, w_key, value_weight, w_output, cache_keys, cache_values,
+    tokens, twisting_table, twist_vec, previous_log_weights, copy_counts,
+):
+    f32, bf16 = jnp.float32, jnp.bfloat16
+    steps, parts, width = activations.shape
+    rows = steps * parts
+    span = cache_keys.shape[1]
+    kvw = w_key.shape[1]
+    qw = w_query.shape[1]
+    groups = kvw // HD
+    pack = steps * (qw // kvw)
+    doms = lax.axis_size("dom")
+    tps = lax.axis_size("tp")
+    middle = HD // 2
+    angles = (span + np.arange(rows) // parts)[:, None] * (
+        500000.0 ** (-2.0 * np.arange(middle) / HD)
+    )
+    cosine = np.concatenate([np.cos(angles)] * 2, 1).astype(np.float32)
+    sine = np.concatenate([-np.sin(angles), np.sin(angles)], 1).astype(np.float32)
+    reward = twisting_table[tokens.reshape(rows)].astype(f32).reshape(rows, 1)
+    vmem = pl.BlockSpec(memory_space=pltpu.VMEM)
+    hbm = pl.BlockSpec(memory_space=pl.ANY)
+    block = jax.ShapeDtypeStruct((doms,) + cache_keys.shape, bf16)
+    attn, all_k, all_v, fresh_sel, out_lw, anc = pl.pallas_call(
+        functools.partial(layer_kernel, steps, parts, doms, tps),
+        out_shape=(
+            jax.ShapeDtypeStruct((rows, width), bf16), block, block,
+            jax.ShapeDtypeStruct((HD, 2 * kvw), bf16),
+            jax.ShapeDtypeStruct((parts, HD), f32),
+            jax.ShapeDtypeStruct((8, HD), jnp.int32),
+        ),
+        in_specs=[hbm, vmem] + [hbm] * 6 + [vmem] * 6,
+        out_specs=(vmem, hbm, hbm, vmem, vmem, vmem),
+        scratch_shapes=[
+            pltpu.VMEM((tps, rows, width), bf16),
+            pltpu.VMEM(w_query.shape, bf16),
+            pltpu.VMEM(w_key.shape, bf16),
+            pltpu.VMEM(value_weight.shape, bf16),
+            pltpu.VMEM(w_output.shape, bf16),
+            pltpu.VMEM(cache_keys.shape, bf16),
+            pltpu.VMEM(cache_values.shape, bf16),
+            pltpu.VMEM((groups, parts, pack, HD), f32),
+            pltpu.VMEM((groups, parts, pack, HD), f32),
+            pltpu.VMEM((groups, parts * pack, span), f32),
+            pltpu.VMEM((rows, qw), bf16),
+            pltpu.VMEM((rows, 2 * kvw), bf16),
+            pltpu.VMEM((doms, rows, 2 * kvw), bf16),
+            pltpu.VMEM((tps - 1, rows, width), f32),
+            pltpu.VMEM((tps - 1, rows, width), f32),
+            pltpu.VMEM((tps, rows, HD), f32),
+            pltpu.VMEM((doms, parts, HD), f32),
+            pltpu.VMEM((doms, parts, HD), f32),
+            pltpu.SemaphoreType.DMA((9,)),
+            pltpu.SemaphoreType.DMA((3 * (tps - 1),)),
+            pltpu.SemaphoreType.DMA((3 * (tps - 1),)),
+            pltpu.SemaphoreType.DMA((3 * (doms - 1),)),
+            pltpu.SemaphoreType.DMA((3 * (doms - 1),)),
+            pltpu.SemaphoreType.DMA((32,)),
+            pltpu.SemaphoreType.DMA((32,)),
+        ],
+        compiler_params=pltpu.CompilerParams(
+            collective_id=0, has_side_effects=True, vmem_limit_bytes=56 << 20
+        ),
+        name="layer",
+    )(
+        activations.reshape(rows, width), norm_gain.reshape(1, -1), w_query, w_key,
+        value_weight, w_output, cache_keys, cache_values, reward, twist_vec.reshape(1, -1),
+        previous_log_weights.reshape(parts, 1), copy_counts.astype(f32).reshape(parts, 1),
+        jnp.asarray(cosine), jnp.asarray(sine),
+    )
+    result = jax.ShapeDtypeStruct((parts, span + steps, kvw), bf16)
+    new_k, new_v = pl.pallas_call(
+        functools.partial(select_kernel, parts, steps),
+        out_shape=(result, result),
+        in_specs=[pl.BlockSpec(memory_space=pltpu.SMEM), vmem, hbm, hbm],
+        out_specs=(vmem, vmem),
+        scratch_shapes=[pltpu.SemaphoreType.DMA((2 * parts,))],
+        name="select",
+    )(anc[0], fresh_sel, all_k, all_v)
+    return attn.reshape(steps, parts, width), new_k, new_v, out_lw[:, 0]
+
+
 def solution(mesh):
+    body = fused if mesh.shape["dom"] == 8 else local
     return jax.shard_map(
-        local,
+        body,
         mesh=mesh,
         in_specs=(
             P(None, "dom", "tp"),

time: 193 us -> 105 us (0.54)
  Pallas kernels: 0 us -> 92.8 us
  blocking collectives: 72.5 us -> 0 us
  waiting for transfers between devices: 46.5 us -> 0 us
  local copies, waits for them, and re-layouts: 32.8 us -> 10.5 us
  between operations: 17.8 us -> 0.69 us
  matrix products: 16.5 us -> 0 us
  other arithmetic: 5.85 us -> 0.68 us
    pallas_call x0 -> x2, Pallas kernels: none -> 92.8 us  [the longest x1 88.6 us: fused(): pl.pallas_call(functools.partial(layer_kernel, steps, parts, doms, tps),...]
    all_gather x2 -> x0, waiting for transfers between devices: 40.9 us -> none  [the longest x1 40.9 us: local(): all_values = lax.all_gather(cache_values, 'dom', axis=0, tiled=True)]
    all_gather x2 -> x0, blocking collectives: 29.4 us -> none  [the longest x1 17.7 us: local(): gathered = lax.all_gather(activations, 'tp', axis=2, tiled=True)]
    psum x2 -> x0, blocking collectives: 21.8 us -> none  [the longest x1 12.6 us: local(): lax.psum(jnp.sum(jnp.exp(particle_log_weight - largest)), 'dom')]
    dot_general x3 -> x0, local copies, waits for them, and re-layouts: 15.5 us -> none  [the longest x1 11.3 us: local(): jnp.dot(flat_rows, w_query, preferred_element_type=jnp.float32)]
    dot_general x5 -> x0, matrix products: 15.5 us -> none  [the longest x1 6.03 us: local(): jnp.dot(flat_rows, w_query, preferred_element_type=jnp.float32)]
    pmax x1 -> x0, blocking collectives: 13.4 us -> none  [local(): largest = lax.pmax(jnp.max(particle_log_weight), 'dom')]
    gather x4 -> x1, local copies, waits for them, and re-layouts: 9.85 us -> 0.8 us  [fused(): reward = twisting_table[tokens.reshape(rows)].astype(f32).reshape(rows, 1)]
  transfers between devices with their start and end apart: 3 -> 0, of which waited for: 2 -> 0; matrix products, arithmetic and copies ran while one was open for 7% -> 0% of each run, Pallas kernels for 0% -> 0%
where the time goes in v2:
time: 105 us
  Pallas kernels  92.8 us (88%)
  local copies, waits for them, and re-layouts  10.5 us (10%)
    pallas_call x1, Pallas kernels, fused(): pl.pallas_call(functools.partial(layer_kernel, steps, parts, doms, tps),...  88.6 us
    unnamed x11, local copies, waits for them, and re-layouts  4.41 us
    pallas_call x1, Pallas kernels, fused(): pl.pallas_call(functools.partial(select_kernel, parts, steps), out_shape=...  4.15 us

profile of v2, /device:TPU:0, one launch (start us, length us, event | category | flops | bytes accessed | tf_op | source)
XLA Modules:
  0.0 104.7 jit_solution(17884517752655881696)
XLA Ops:
  0.6 0.0 copy-start
  0.6 0.8 reshape.69
  1.5 0.7 convert_bitcast_fusion
  2.1 0.0 copy-done
  2.1 0.8 gather_fusion
  2.9 0.7 copy.26.counts
  3.6 1.3 %copy.25.prev = f32[16,1]{1,0:T(8,128)} copy(f32[16,1]{0,1:T(1,128)} %bitcast.18) | data formatting | bytes 128 | tf_op jit(solution)/shard_map/reshape | solution.py:511
  4.9 0.7 copy.24.reward
  5.7 88.6 %layer.1 = (bf16[64,1024]{1,0:T(8,128)(2,1)}, bf16[8,16,128,256]{3,2,1,0:T(8,128)(2,1)}, bf16[8,16,128,256]{3,2,1,0:T(8,128)(2,1)}, bf16[128,512]{1,0:T(8,128)(2...) custom-call(bf16[64,1024]{1,0:T(8,128)(2,1)} %bitcast.14, f32[1,4096]{1,0:T(1,128)} %bitcast.16, bf16[4096,1024]{1,0:T(8,128)(2,1)} %wq.1, ...), custom_call_target="tpu_custom_call" | custom-call | tf_op jit(solution)/shard_map/layer/pallas_call | solution.py:467
  94.3 1.2 %slice_bitcast_fusion.anc = s32[128]{0:T(128)} fusion(s32[8,128]{1,0:T(8,128)} %get-tuple-element.13), kind=kLoop, calls=%fused_computation.6 | loop fusion | bytes 1024 | tf_op jit(solution)/shard_map/squeeze | solution.py:522
  95.5 4.1 %select.1 = (bf16[16,132,256]{2,1,0:T(8,128)(2,1)}, bf16[16,132,256]{2,1,0:T(8,128)(2,1)}) custom-call(s32[128]{0:T(128)} %slice_bitcast_fusion.anc, bf16[128,512]{1,0:T(8,128)(2,1)} %get-tuple-element.14.fresh_sel, bf16[8,16,128,256]{3,2,1,0:T(8,128)(2,1)} %get-tuple-element.15.all_k, bf16[8,16,128,256]{3,2,1,0:T(8,128)(2,1)} %get-tuple-element.16.all_v), custom_call_target="tpu_custom_call" | custom-call | tf_op jit(solution)/shard_map/select/pallas_call | solution.py:515
  99.6 0.0 copy-start.3
  99.6 0.0 copy-start.1
  99.7 0.0 copy-start.2
  99.7 2.5 %copy.27 = bf16[16,132,256]{2,0,1:T(8,128)(2,1)} copy(bf16[16,132,256]{2,1,0:T(8,128)(2,1)} %get-tuple-element.25) | data formatting | bytes 2162688
  102.2 0.0 copy-done.3
  102.2 0.6 slice_reduce_fusion
  102.8 0.0 copy-done.1
  102.8 1.2 %copy.28 = bf16[16,132,256]{2,0,1:T(8,128)(2,1)} copy(bf16[16,132,256]{2,1,0:T(8,128)(2,1)S(1)} %copy-done.1) | data formatting | bytes 2162688
  104.0 0.0 copy-done.2
  104.0 0.7 copy.30
  (3 shorter events, 0.0 us)
Async XLA Ops:
  0.6 1.5 %copy-start = (bf16[128256]{0:T(1024)(128)(2,1)S(1)}, bf16[128256]{0:T(1024)(128)(2,1)}, u32[]{:S(2)}) copy-start(bf16[128256]{0:T(1024)(128)(2,1)} %param.24) | copy-start | bytes 769540
  99.6 2.6 %copy-start.3 = (f32[16,128]{1,0:T(8,128)S(1)}, f32[16,128]{1,0:T(8,128)}, u32[]{:S(2)}) copy-start(f32[16,128]{1,0:T(8,128)} %get-tuple-element.19) | copy-start | bytes 24580
  99.6 3.2 %copy-start.1 = (bf16[16,132,256]{2,1,0:T(8,128)(2,1)S(1)}, bf16[16,132,256]{2,1,0:T(8,128)(2,1)}, u32[]{:S(2)}) copy-start(bf16[16,132,256]{2,1,0:T(8,128)(2,1)} %get-tuple-element.26) | copy-start | bytes 3244036
  99.7 4.4 %copy-start.2 = (bf16[64,1024]{1,0:T(8,128)(2,1)S(1)}, bf16[64,1024]{1,0:T(8,128)(2,1)}, u32[]{:S(2)}) copy-start(bf16[64,1024]{1,0:T(8,128)(2,1)} %get-tuple-element.12) | copy-start | bytes 393220

commit v3 on v2

--- a/solution.py
+++ b/solution.py
@@ -135,7 +135,7 @@
 
 def layer_kernel(
     steps, parts, doms, tps,
-    act, gain, wq, wk, wv, wo, ck, cv, reward, twist, prev, counts, cosine, sine,
+    act, gain, wq, wk, wv, wo, ck, cv, twist, aux, cosine, sine,
     attn_out, all_k, all_v, fresh_sel, out_lw, anc_out,
     act_all, wq_v, wk_v, wv_v, wo_v, ck_v, cv_v, qs, cx, sc1, ctx_b, fresh, fresh_all,
     rs_send, rs_recv, sc_all, lw_all, cnt_all,
@@ -181,7 +181,7 @@
     load_cv = fetch(5, cv, cv_v)
     load_o = fetch(6, wo, wo_v)
 
-    cnt_all[me_d] = jnp.broadcast_to(counts[...], cnt_all.shape[1:])
+    cnt_all[me_d] = jnp.broadcast_to(aux[:, 1:], cnt_all.shape[1:])
     pl.semaphore_wait(barrier, tps + doms - 2)
 
     def tp_push(base, k, src, dst):
@@ -324,6 +324,21 @@
         rs_send[k - 1] = mix((me_t + k) % tps)
         sums.append(tp_push(tps - 1, k, rs_send.at[k - 1], rs_recv.at[k - 1]))
     head = mix(me_t)
+
+    def done(kind, h):
+        for which in range(2):
+            moves[kind, h, which].wait_recv()
+
+    def relay(kind, to, h, slot):
+        for which in range(2):
+            moves[kind, h, which] = piece(kind, to, which, h, slot, False)
+
+    done(0, 0)
+    relay(2, yn, 0, xn)
+    relay(4, sib, 0, xn)
+    done(1, 1)
+    relay(6, xn, 1, yn)
+    relay(5, sib, 1, yn)
     for k in range(1, tps):
         sums[k - 1].wait()
         head = head + rs_recv[k - 1]
@@ -341,30 +356,16 @@
     both = sc_all[0]
     for t in range(1, tps):
         both = both + sc_all[t]
-    score = reward[...] + both[:, :1] / jnp.sqrt(both[:, HD - 1 :] / (width * tps) + 1e-06)
+    score = both[:, :1] / jnp.sqrt(both[:, HD - 1 :] / (width * tps) + 1e-06)
     total = score[:parts]
     for s in range(1, steps):
         total = total + score[s * parts : (s + 1) * parts]
-    mine = jnp.broadcast_to(prev[...] + total, (parts, HD))
+    mine = jnp.broadcast_to(aux[:, :1] + total, (parts, HD))
     lw_all[me_d] = mine
     lws = [
         dom_push(2 * (doms - 1), k, lw_all.at[me_d], lw_all.at[me_d]) for k in range(1, doms)
     ]
 
-    def done(kind, h):
-        for which in range(2):
-            moves[kind, h, which].wait_recv()
-
-    def relay(kind, to, h, slot):
-        for which in range(2):
-            moves[kind, h, which] = piece(kind, to, which, h, slot, False)
-
-    done(0, 0)
-    relay(2, yn, 0, xn)
-    relay(4, sib, 0, xn)
-    done(1, 1)
-    relay(6, xn, 1, yn)
-    relay(5, sib, 1, yn)
     done(0, 1)
     relay(4, sib, 1, xn)
     done(1, 0)
@@ -425,7 +426,7 @@
     width = all_k.shape[3]
     copies = []
     for i in range(parts):
-        a = anc[i]
+        a = anc[0, i]
         d, n = a // parts, a % parts
         for which, (src, dst) in enumerate(((all_k, new_k), (all_v, new_v))):
             copy = pltpu.make_async_copy(
@@ -460,7 +461,8 @@
     )
     cosine = np.concatenate([np.cos(angles)] * 2, 1).astype(np.float32)
     sine = np.concatenate([-np.sin(angles), np.sin(angles)], 1).astype(np.float32)
-    reward = twisting_table[tokens.reshape(rows)].astype(f32).reshape(rows, 1)
+    reward = jnp.sum(twisting_table[tokens].astype(f32), 0)
+    aux = jnp.stack([previous_log_weights + reward, copy_counts.astype(f32)], 1)
     vmem = pl.BlockSpec(memory_space=pltpu.VMEM)
     hbm = pl.BlockSpec(memory_space=pl.ANY)
     block = jax.ShapeDtypeStruct((doms,) + cache_keys.shape, bf16)
@@ -472,7 +474,7 @@
             jax.ShapeDtypeStruct((parts, HD), f32),
             jax.ShapeDtypeStruct((8, HD), jnp.int32),
         ),
-        in_specs=[hbm, vmem] + [hbm] * 6 + [vmem] * 6,
+        in_specs=[hbm, vmem] + [hbm] * 6 + [vmem] * 4,
         out_specs=(vmem, hbm, hbm, vmem, vmem, vmem),
         scratch_shapes=[
             pltpu.VMEM((tps, rows, width), bf16),
@@ -507,8 +509,7 @@
         name="layer",
     )(
         activations.reshape(rows, width), norm_gain.reshape(1, -1), w_query, w_key,
-        value_weight, w_output, cache_keys, cache_values, reward, twist_vec.reshape(1, -1),
-        previous_log_weights.reshape(parts, 1), copy_counts.astype(f32).reshape(parts, 1),
+        value_weight, w_output, cache_keys, cache_values, twist_vec.reshape(1, -1), aux,
         jnp.asarray(cosine), jnp.asarray(sine),
     )
     result = jax.ShapeDtypeStruct((parts, span + steps, kvw), bf16)
@@ -519,7 +520,7 @@
         out_specs=(vmem, vmem),
         scratch_shapes=[pltpu.SemaphoreType.DMA((2 * parts,))],
         name="select",
-    )(anc[0], fresh_sel, all_k, all_v)
+    )(anc, fresh_sel, all_k, all_v)
     return attn.reshape(steps, parts, width), new_k, new_v, out_lw[:, 0]
 
 

time: 105 us -> 104 us (level)
  local copies, waits for them, and re-layouts: 10.5 us -> 7.38 us
  other arithmetic: 0.68 us -> 2.09 us
    reshape x3 -> x0, local copies, waits for them, and re-layouts: 2.82 us -> none  [the longest x1 1.33 us: fused(): previous_log_weights.reshape(parts, 1)]
    another operation x0 -> x3, other arithmetic: none -> 1.37 us  [fused(): aux = jnp.stack([previous_log_weights + reward, copy_counts.astype(f32)], 1)]
    squeeze x1 -> x0, local copies, waits for them, and re-layouts: 1.19 us -> none  [fused(): anc[0]]
    unnamed x11 -> x9, local copies, waits for them, and re-layouts: 4.41 us -> 4.4 us
where the time goes in v3:
time: 104 us
  Pallas kernels  93.4 us (90%)
  local copies, waits for them, and re-layouts  7.38 us (7%)
  other arithmetic  2.09 us (2%)
    pallas_call x1, Pallas kernels, fused(): pl.pallas_call(functools.partial(layer_kernel, steps, parts, doms, tps),...  89.2 us
    unnamed x9, local copies, waits for them, and re-layouts  4.4 us
    pallas_call x1, Pallas kernels, fused(): pl.pallas_call(functools.partial(select_kernel, parts, steps), out_shape=...  4.17 us

profile of v3, /device:TPU:0, one launch (start us, length us, event | category | flops | bytes accessed | tf_op | source)
XLA Modules:
  0.0 103.5 jit_solution(16041607396230409005)
XLA Ops:
  0.6 0.0 copy-start
  0.6 0.7 convert_bitcast_fusion
  1.3 0.7 compare_select_fusion
  2.0 0.1 reshape.26
  2.1 0.0 copy-done
  2.1 0.8 gather_fusion
  2.9 0.1 reshape.34
  3.0 0.7 add_bitcast_fusion
  3.7 0.7 copy.27.aux
  4.4 89.2 %layer.1 = (bf16[64,1024]{1,0:T(8,128)(2,1)}, bf16[8,16,128,256]{3,2,1,0:T(8,128)(2,1)}, bf16[8,16,128,256]{3,2,1,0:T(8,128)(2,1)}, bf16[128,512]{1,0:T(8,128)(2...) custom-call(bf16[64,1024]{1,0:T(8,128)(2,1)} %bitcast.8, f32[1,4096]{1,0:T(1,128)} %bitcast.10, bf16[4096,1024]{1,0:T(8,128)(2,1)} %wq.1, ...), custom_call_target="tpu_custom_call" | custom-call | tf_op jit(solution)/shard_map/layer/pallas_call | solution.py:469
  93.6 1.3 %slice_reduce_fusion = f32[16]{0:T(128)} fusion(f32[16,128]{1,0:T(8,128)} %get-tuple-element.19), kind=kLoop, calls=%fused_computation.1 | loop fusion | bytes 128 | tf_op jit(solution)/shard_map/slice | solution.py:524
  94.9 4.2 %select.1 = (bf16[16,132,256]{2,1,0:T(8,128)(2,1)}, bf16[16,132,256]{2,1,0:T(8,128)(2,1)}) custom-call(s32[8,128]{1,0:T(8,128)} %get-tuple-element.13.anc, bf16[128,512]{1,0:T(8,128)(2,1)} %get-tuple-element.14.fresh_sel, bf16[8,16,128,256]{3,2,1,0:T(8,128)(2,1)} %get-tuple-element.15.all_k, bf16[8,16,128,256]{3,2,1,0:T(8,128)(2,1)} %get-tuple-element.16.all_v), custom_call_target="tpu_custom_call" | custom-call | tf_op jit(solution)/shard_map/select/pallas_call | solution.py:516
  99.1 0.0 copy-start.1
  99.1 0.0 copy-start.2
  99.1 2.5 %copy.28 = bf16[16,132,256]{2,0,1:T(8,128)(2,1)} copy(bf16[16,132,256]{2,1,0:T(8,128)(2,1)} %get-tuple-element.29) | data formatting | bytes 2162688
  101.7 0.0 copy-done.1
  101.7 1.2 %copy.29 = bf16[16,132,256]{2,0,1:T(8,128)(2,1)} copy(bf16[16,132,256]{2,1,0:T(8,128)(2,1)S(1)} %copy-done.1) | data formatting | bytes 2162688
  102.9 0.0 copy-done.2
  102.9 0.7 copy.31
  (3 shorter events, 0.0 us)
Async XLA Ops:
  0.6 1.5 %copy-start = (bf16[128256]{0:T(1024)(128)(2,1)S(1)}, bf16[128256]{0:T(1024)(128)(2,1)}, u32[]{:S(2)}) copy-start(bf16[128256]{0:T(1024)(128)(2,1)} %param.24) | copy-start | bytes 769540
  99.1 2.6 %copy-start.1 = (bf16[16,132,256]{2,1,0:T(8,128)(2,1)S(1)}, bf16[16,132,256]{2,1,0:T(8,128)(2,1)}, u32[]{:S(2)}) copy-start(bf16[16,132,256]{2,1,0:T(8,128)(2,1)} %get-tuple-element.30) | copy-start | bytes 3244036
  99.1 3.7 %copy-start.2 = (bf16[64,1024]{1,0:T(8,128)(2,1)S(1)}, bf16[64,1024]{1,0:T(8,128)(2,1)}, u32[]{:S(2)}) copy-start(bf16[64,1024]{1,0:T(8,128)(2,1)} %get-tuple-element.12) | copy-start | bytes 393220
